TPU v7x, 512 devices: a whole 4x8x8 slice. The times are simulated.
512 devices in a mesh: dp: 8 (over y_hi, core), expert: 64 (over y_lo, x, z).
Axes of the slice: x: 4, y: 8 (y_hi: 4, y_lo: 2; y = y_hi * 2 + y_lo), z: 8, core: 2. Of those that a mesh axis runs over, the one named last changes fastest.
Arguments:
- weights: bfloat16 [16, 3584, 512], P(None, ('dp', 'expert')), may hold values from -0.09375 to 0.09375
- first_moment: float32 [16, 3584, 512], P(None, ('dp', 'expert')), may hold values from -3 to 3
- second_moment: float32 [16, 3584, 512], P(None, ('dp', 'expert')), may hold values from 0.05 to 2
- placement: int32 [64], replicated, may hold values from 0 to 15, as said below
- block_counts: int32 [8, 64], P('dp', 'expert'), may hold values from 1 to 2
- tokens: bfloat16 [8, 64, 256, 3584], P('dp', 'expert'), may hold values from -6 to 6
- hidden_grad: bfloat16 [8, 64, 256, 256], P('dp', 'expert'), may hold values from -1.1953125 to 1.1953125
Outputs:
- new_weights: bfloat16 [64, 3584, 512], P('expert', 'dp')
- new_first: float32 [64, 3584, 512], P('expert', 'dp')
- new_second: float32 [64, 3584, 512], P('expert', 'dp')
Inputs may be any that keep to these rules, and one draw needn't show every extreme that they name: `placement`: every expert block 0 to 15 is owned by at least one device. `block_counts`: the rows after a device's live blocks are padding.
All inputs are finite; a program needn't handle non-finite values.
Results may differ from a plain program's by a relative error of at most 0.015.
Values may be sent and summed in bfloat16 or wider, within the bound.
No kernel may reach another device: no remote copies, remote signals or barrier semaphores. Data moves between devices by JAX's collectives and lax.ppermute only.
A program may use at most 64 MiB of HBM per device.

v0:
```python
import jax
import jax.numpy as jnp
from jax import lax
from jax.sharding import PartitionSpec as P

BLOCK = 128
beta_first = 0.9
beta_second = 0.95
learning_rate = 0.001
weight_decay = 0.1
adam_epsilon = 1e-08
adam_steps = 10.0


def silu_grads(projected, upstream, live_mask):
    half_width = projected.shape[1] // 2
    gate_part = projected[:, :half_width]
    upward = projected[:, half_width:]
    sigmoid_gate = jax.nn.sigmoid(gate_part)
    masked = jnp.where(live_mask, upstream.astype(jnp.float32), 0.0)
    grad_gate = masked * upward * sigmoid_gate * (1.0 + gate_part * (1.0 - sigmoid_gate))
    grad_upward = masked * gate_part * sigmoid_gate
    return jnp.concatenate([grad_gate, grad_upward], axis=1).astype(jnp.bfloat16)


def adam_update(params, first_moment, second_moment, gradient):
    moment_one = beta_first * first_moment + (1.0 - beta_first) * gradient
    moment_two = beta_second * second_moment + (1.0 - beta_second) * gradient * gradient
    correct_one = 1.0 - beta_first**adam_steps
    correct_two = 1.0 - beta_second**adam_steps
    params_full = params.astype(jnp.float32)
    step_size = (
        moment_one / correct_one / (jnp.sqrt(moment_two / correct_two) + adam_epsilon)
        + weight_decay * params_full
    )
    return ((params_full - learning_rate * step_size).astype(jnp.bfloat16), moment_one, moment_two)


def on_device(weights, first_moment, second_moment, placement, block_counts, tokens, hidden_grad):
    expert_count = lax.axis_size("expert")
    block_total = weights.shape[0]
    span_rows = weights.shape[1]
    col_total = weights.shape[2]
    inputs = tokens[0, 0]
    row_total = inputs.shape[0]
    narrow = jnp.bfloat16
    live_mask = (jnp.arange(row_total) < BLOCK * block_counts[0, 0])[:, None]
    own_shape = (expert_count * span_rows, col_total)
    pick = (placement[:, None] == jnp.arange(block_total)[None, :]).astype(narrow)
    same = (placement[:, None] == placement[None, :]).astype(narrow)

    def exchange(values):
        return lax.all_to_all(values, "expert", split_axis=0, concat_axis=0, tiled=True)

    def spread(stored):
        return jnp.einsum("ju,urc->jrc", pick, stored, preferred_element_type=jnp.float32).astype(
            narrow
        )

    arrived = exchange(spread(weights))
    own_rows = arrived.reshape(own_shape)
    gathered = lax.all_gather(own_rows, "dp", axis=0, tiled=True)
    moments = jnp.concatenate([first_moment, second_moment], axis=1).astype(narrow)
    moments_sent, _ = lax.optimization_barrier((spread(moments), arrived))
    moments_here = exchange(moments_sent)
    gathered, moments_here = lax.optimization_barrier((gathered, moments_here))
    projected = jnp.dot(inputs, gathered, preferred_element_type=jnp.float32)
    grad_proj = silu_grads(projected, hidden_grad[0, 0], live_mask)
    term = lax.dot_general(
        inputs, grad_proj, (((0,), (0,)), ((), ())), preferred_element_type=jnp.float32
    ).astype(narrow)
    summed_data = lax.psum_scatter(term, "dp", scatter_dimension=0, tiled=True)
    at_home = exchange(summed_data.reshape(expert_count, span_rows, col_total))
    block_grad = jnp.einsum(
        "jk,krc->jrc", same, at_home, preferred_element_type=jnp.float32
    ).astype(narrow)
    grad_here = exchange(block_grad)
    updated, moment_one, moment_two = adam_update(
        own_rows,
        moments_here[:, :span_rows].reshape(own_shape).astype(jnp.float32),
        moments_here[:, span_rows:].reshape(own_shape).astype(jnp.float32),
        grad_here.reshape(own_shape).astype(jnp.float32),
    )
    return (updated[None], moment_one[None], moment_two[None])


def solution(mesh):
    in_specs = (
        P(None, ("dp", "expert"), None),
        P(None, ("dp", "expert"), None),
        P(None, ("dp", "expert"), None),
        P(),
        P("dp", "expert"),
        P("dp", "expert", None, None),
        P("dp", "expert", None, None),
    )
    out_specs = (P("expert", "dp", None), P("expert", "dp", None), P("expert", "dp", None))
    return jax.shard_map(
        on_device, mesh=mesh, in_specs=in_specs, out_specs=out_specs, check_vma=False
    )
```

profile of v0, /device:TPU:16, one launch (start us, length us, event | category | flops | bytes accessed | tf_op | source)
XLA Modules:
  0.0 233.5 jit_solution(11896177370033334054)
XLA Ops:
  7.3 1.4 convolution_convert_fusion.2
  8.9 33.6 %all_to_all.20 = bf16[64,7,512]{2,1,0:T(8,128)(2,1)S(1)} all-to-all(bf16[64,7,512]{2,1,0:T(8,128)(2,1)S(1)} %copy.20), channel_id=1, replica_groups=mesh['dp'=8,'expert'=64] {'expert'}, dimensions={0} | all-to-all | bytes 917504 | tf_op jit(solution)/shard_map/all_to_all | solution.py:53
  42.5 0.9 reshape.142
  43.5 0.4 convolution_convert_fusion.1
  44.0 1.5 copy.21
  45.5 4.7 %all-to-all-start.1 = ((bf16[64,14,512]{2,1,0:T(8,128)(2,1)}), bf16[64,14,512]{2,1,0:T(8,128)(2,1)S(1)}, u32[]{:S(2)}, u32[]{:S(2)}) async-start(bf16[64,14,512]{2,1,0:T(8,128)(2,1)} %copy.21), calls=%async_computation.1 | async-start | bytes 2097152 | tf_op jit(solution)/shard_map/all_to_all | solution.py:53
  50.2 1.0 copy.22
  51.9 33.5 %all-to-all-done.1 = bf16[64,14,512]{2,1,0:T(8,128)(2,1)S(1)} async-done(((bf16[64,14,512]{2,1,0:T(8,128)(2,1)}), bf16[64,14,512]{2,1,0:T(8,128)(2,1)S(1)}, u32[]{:S(2)}, u32[]{:S(2)}) %all-to-all-start.1) | async-done | bytes 917536 | tf_op jit(solution)/shard_map/all_to_all | solution.py:53
  85.4 9.9 %all-gather.2.cloned.1.call-done = bf16[3584,512]{1,0:T(8,128)(2,1)} async-done(((bf16[448,512]{1,0:T(8,128)(2,1)}), bf16[3584,512]{1,0:T(8,128)(2,1)}) %all-gather.2.cloned.1.call-update) | async-done | bytes 3670032 | tf_op jit(solution)/shard_map/all_gather | solution.py:62
  95.3 3.2 %fusion.4 = f32[256,512]{0,1:T(8,128)S(1)} fusion(bf16[3584,512]{1,0:T(8,128)(2,1)} %all-gather.2.cloned.1.call-done, bf16[1,1,256,3584]{3,2,1,0:T(8,128)(2,1)S(1)} %copy-done), kind=kOutput, calls=%fused_computation.9 | convolution fusion | flops 939524096 | bytes 6029312 | tf_op jit(solution)/shard_map/dot_general | solution.py:67
  98.7 3.0 %fusion = bf16[3584,512]{0,1:T(8,128)(2,1)} fusion(bf16[1,1,256,3584]{3,2,1,0:T(8,128)(2,1)S(1)} %copy-done, bf16[256,256]{0,1:T(8,128)(2,1)S(1)} %get-tuple-element.15, bf16[256,256]{0,1:T(8,128)(2,1)S(1)} %get-tuple-element.14), kind=kOutput, calls=%fused_computation.1 | convolution fusion | flops 941883392 | bytes 5767168 | tf_op jit(solution)/shard_map/dot_general | solution.py:69
  101.6 6.0 %copy.26 = bf16[3584,512]{1,0:T(8,128)(2,1)} copy(bf16[3584,512]{0,1:T(8,128)(2,1)} %fusion) | data formatting | bytes 7340032
  107.6 52.1 %reduce-scatter.4.cloned.1.call-done = bf16[448,512]{1,0:T(8,128)(2,1)} async-done(((bf16[3584,512]{1,0:T(8,128)(2,1)}), bf16[448,512]{1,0:T(8,128)(2,1)}) %reduce-scatter.4.cloned.1.call-update) | async-done | bytes 458768 | tf_op jit(solution)/shard_map/reduce_scatter | solution.py:72
  159.7 2.0 reshape.143
  161.7 31.4 %all_to_all.21 = bf16[64,7,512]{2,1,0:T(8,128)(2,1)S(1)} all-to-all(bf16[64,7,512]{2,1,0:T(8,128)(2,1)} %reshape.143), channel_id=1, replica_groups=mesh['dp'=8,'expert'=64] {'expert'}, dimensions={0} | all-to-all | bytes 917504 | tf_op jit(solution)/shard_map/all_to_all | solution.py:53
  193.4 1.1 copy.25
  194.5 6.6 %all-to-all-start.3 = ((bf16[64,7,512]{2,1,0:T(8,128)(2,1)}), bf16[64,7,512]{2,1,0:T(8,128)(2,1)}, u32[]{:S(2)}, u32[]{:S(2)}) async-start(bf16[64,7,512]{2,1,0:T(8,128)(2,1)} %copy.25), calls=%async_computation.3 | async-start | bytes 1048576 | tf_op jit(solution)/shard_map/all_to_all | solution.py:53
  201.0 1.1 reshape.144
  202.1 1.6 convert_multiply_fusion
  203.7 2.4 %mul.128 = f32[1,448,512]{2,1,0:T(8,128)} reshape(f32[64,7,512]{2,1,0:T(8,128)} %get-tuple-element.13) | data formatting | bytes 1835008 | tf_op jit(solution)/shard_map/mul | solution.py:27
  206.1 2.3 mul.138
  208.4 12.5 %all-to-all-done.3 = bf16[64,7,512]{2,1,0:T(8,128)(2,1)} async-done(((bf16[64,7,512]{2,1,0:T(8,128)(2,1)}), bf16[64,7,512]{2,1,0:T(8,128)(2,1)}, u32[]{:S(2)}, u32[]{:S(2)}) %all-to-all-start.3) | async-done | bytes 458784 | tf_op jit(solution)/shard_map/all_to_all | solution.py:53
  220.9 2.1 reshape.146
  223.0 3.6 %subtract_convert_fusion = (bf16[1,448,512]{2,1,0:T(8,128)(2,1)}, f32[1,448,512]{2,1,0:T(8,128)}, f32[1,448,512]{2,1,0:T(8,128)}) fusion(f32[1,448,512]{2,1,0:T(8,128)S(1)} %copy-done.1, f32[1,448,512]{2,1,0:T(8,128)} %mul.128, f32[1,448,512]{2,1,0:T(8,128)} %reshape.146, f32[1,448,512]{2,1,0:T(8,128)} %mul.138), kind=kLoop, calls=%fused_computation.13 | loop fusion | flops 3211264 | bytes 5963776 | tf_op jit(solution)/shard_map/convert_element_type | solution.py:36
  (20 shorter events, 0.9 us)
Async XLA Ops:
  7.2 88.2 %copy-start = (bf16[1,1,256,3584]{3,2,1,0:T(8,128)(2,1)S(1)}, bf16[1,1,256,3584]{3,2,1,0:T(8,128)(2,1)}, u32[]{:S(2)}) copy-start(bf16[1,1,256,3584]{3,2,1,0:T(8,128)(2,1)} %param.12) | copy-start | bytes 5505028
  7.2 36.4 %copy-start.4 = (s32[64]{0:T(128)S(1)}, s32[64]{0:T(128)}, u32[]{:S(2)}) copy-start(s32[64]{0:T(128)} %param.10) | copy-start | bytes 772
  7.2 36.3 %copy-start.2 = (f32[16,7,512]{2,0,1:T(8,128)S(1)}, f32[16,7,512]{2,0,1:T(8,128)}, u32[]{:S(2)}) copy-start(f32[16,7,512]{2,0,1:T(8,128)} %param.8) | copy-start | bytes 688132
  7.2 36.3 %copy-start.3 = (f32[16,7,512]{2,0,1:T(8,128)S(1)}, f32[16,7,512]{2,0,1:T(8,128)}, u32[]{:S(2)}) copy-start(f32[16,7,512]{2,0,1:T(8,128)} %param.9) | copy-start | bytes 688132
  7.2 88.1 %all-gather.2.cloned.1.call-start = ((), (), s32[]{:S(2)}) async-start(), calls=%async_computation.5 | async-start | bytes 4128768 | tf_op jit(solution)/shard_map/all_gather | solution.py:62
  45.5 39.9 %all-to-all-start.1 = ((bf16[64,14,512]{2,1,0:T(8,128)(2,1)}), bf16[64,14,512]{2,1,0:T(8,128)(2,1)S(1)}, u32[]{:S(2)}, u32[]{:S(2)}) async-start(bf16[64,14,512]{2,1,0:T(8,128)(2,1)} %copy.21), calls=%async_computation.1 | async-start | bytes 2097152 | tf_op jit(solution)/shard_map/all_to_all | solution.py:53
  50.2 109.5 %reduce-scatter.4.cloned.1.call-start = ((), (), s32[]{:S(2)}) async-start(), calls=%async_computation.6 | async-start | bytes 4128768 | tf_op jit(solution)/shard_map/reduce_scatter | solution.py:72
  194.5 26.5 %all-to-all-start.3 = ((bf16[64,7,512]{2,1,0:T(8,128)(2,1)}), bf16[64,7,512]{2,1,0:T(8,128)(2,1)}, u32[]{:S(2)}, u32[]{:S(2)}) async-start(bf16[64,7,512]{2,1,0:T(8,128)(2,1)} %copy.25), calls=%async_computation.3 | async-start | bytes 1048576 | tf_op jit(solution)/shard_map/all_to_all | solution.py:53
  203.7 19.3 %copy-start.1 = (f32[1,448,512]{2,1,0:T(8,128)S(1)}, f32[1,448,512]{2,1,0:T(8,128)}, u32[]{:S(2)}) copy-start(f32[1,448,512]{2,1,0:T(8,128)} %reshape.144) | copy-start | bytes 2752516
Sparse Core Ops, SparseCore 0:
  43.6 51.6 all-gather.1
  107.8 51.8 reduce-scatter.3
where the time goes:
time: 234 us; the launch traced here: 233 us
  waiting for transfers between devices  108 us (46%)
  blocking collectives  65 us (28%)
  local copies, waits for them, and re-layouts  20.5 us (9%)
  between operations  14.8 us (6%)
  starting transfers between devices  11.3 us (5%)
  matrix products  8.32 us (4%)
  other arithmetic  5.46 us (2%)
    all_to_all x2, blocking collectives, exchange(): lax.all_to_all(values, 'expert', split_axis=0, concat_axis=0, tiled=True)  65 us
    reduce_scatter x1, waiting for transfers between devices, on_device(): summed_data = lax.psum_scatter(term, 'dp', scatter_dimension=0, tiled=True)  52.1 us
    all_to_all x2, waiting for transfers between devices, exchange(): lax.all_to_all(values, 'expert', split_axis=0, concat_axis=0, tiled=True)  46 us
    all_to_all x2, starting transfers between devices, exchange(): lax.all_to_all(values, 'expert', split_axis=0, concat_axis=0, tiled=True)  11.2 us
    all_gather x1, waiting for transfers between devices, on_device(): gathered = lax.all_gather(own_rows, 'dp', axis=0, tiled=True)  9.94 us
    unnamed x12, local copies, waits for them, and re-layouts  7.01 us
  transfers between devices with their start and end apart: 4, of which 4 were waited for; matrix products, arithmetic and copies ran while one was open for 4% of the time, Pallas kernels for 0%

commit v1 on v0

--- a/solution.py
+++ b/solution.py
@@ -59,7 +59,9 @@
 
     arrived = exchange(spread(weights))
     own_rows = arrived.reshape(own_shape)
-    gathered = lax.all_gather(own_rows, "dp", axis=0, tiled=True)
+    gathered = jnp.concatenate(
+        lax.all_to_all(jnp.stack([own_rows] * lax.axis_size("dp")), "dp", 0, 0), axis=0
+    )
     moments = jnp.concatenate([first_moment, second_moment], axis=1).astype(narrow)
     moments_sent, _ = lax.optimization_barrier((spread(moments), arrived))
     moments_here = exchange(moments_sent)

time: 234 us -> 305 us (1.30)
  waiting for transfers between devices: 108 us -> 184 us
  blocking collectives: 65 us -> 31.4 us
  starting transfers between devices: 11.3 us -> 32.6 us
  local copies, waits for them, and re-layouts: 20.5 us -> 24.5 us
    all_to_all x0 -> x1, waiting for transfers between devices: none -> 81.8 us  [on_device(): lax.all_to_all(jnp.stack([own_rows] * lax.axis_size('dp')), 'dp', 0, 0)]
    all_to_all x2 -> x1, blocking collectives: 65 us -> 31.4 us  [exchange(): lax.all_to_all(values, 'expert', split_axis=0, concat_axis=0, tiled=True)]
    all_to_all x2 -> x3, starting transfers between devices: 11.2 us -> 26.1 us  [exchange(): lax.all_to_all(values, 'expert', split_axis=0, concat_axis=0, tiled=True)]
    all_to_all x2 -> x3, waiting for transfers between devices: 46 us -> 57.6 us  [exchange(): lax.all_to_all(values, 'expert', split_axis=0, concat_axis=0, tiled=True)]
    all_gather x1 -> x0, waiting for transfers between devices: 9.94 us -> none  [on_device(): gathered = lax.all_gather(own_rows, 'dp', axis=0, tiled=True)]
    reduce_scatter x1, waiting for transfers between devices: 52.1 us -> 44.9 us  [on_device(): summed_data = lax.psum_scatter(term, 'dp', scatter_dimension=0, tiled=True)]
    all_to_all x0 -> x1, starting transfers between devices: none -> 6.53 us  [on_device(): lax.all_to_all(jnp.stack([own_rows] * lax.axis_size('dp')), 'dp', 0, 0)]
    another operation x0 -> x2, local copies, waits for them, and re-layouts: none -> 4.09 us  [on_device(): jnp.stack([own_rows] * lax.axis_size('dp'))]
  transfers between devices with their start and end apart: 4 -> 5, of which waited for: 4 -> 5; matrix products, arithmetic and copies ran while one was open for 4% -> 4% of each run, Pallas kernels for 0% -> 0%
where the time goes in v1:
time: 305 us; the launch traced here: 304 us
  waiting for transfers between devices  184 us (60%)
  starting transfers between devices  32.6 us (11%)
  blocking collectives  31.4 us (10%)
  local copies, waits for them, and re-layouts  24.5 us (8%)
  between operations  14.8 us (5%)
  matrix products  8.93 us (3%)
  other arithmetic  7.32 us (2%)
    all_to_all x1, waiting for transfers between devices, on_device(): lax.all_to_all(jnp.stack([own_rows] * lax.axis_size('dp')), 'dp', 0, 0)  81.8 us
    all_to_all x3, waiting for transfers between devices, exchange(): lax.all_to_all(values, 'expert', split_axis=0, concat_axis=0, tiled=True)  57.6 us
    reduce_scatter x1, waiting for transfers between devices, on_device(): summed_data = lax.psum_scatter(term, 'dp', scatter_dimension=0, tiled=True)  44.9 us
    all_to_all x1, blocking collectives, exchange(): lax.all_to_all(values, 'expert', split_axis=0, concat_axis=0, tiled=True)  31.4 us
    all_to_all x3, starting transfers between devices, exchange(): lax.all_to_all(values, 'expert', split_axis=0, concat_axis=0, tiled=True)  26.1 us
    unnamed x8, local copies, waits for them, and re-layouts  6.99 us
    all_to_all x1, starting transfers between devices, on_device(): lax.all_to_all(jnp.stack([own_rows] * lax.axis_size('dp')), 'dp', 0, 0)  6.53 us
  transfers between devices with their start and end apart: 5, of which 5 were waited for; matrix products, arithmetic and copies ran while one was open for 4% of the time, Pallas kernels for 0%

profile of v1, /device:TPU:16, one launch (start us, length us, event | category | flops | bytes accessed | tf_op | source)
XLA Modules:
  0.0 303.7 jit_solution(15244670176033276123)
XLA Ops:
  7.2 1.4 convolution_convert_fusion.2
  9.6 14.8 %all-to-all-start = ((bf16[64,7,512]{2,1,0:T(8,128)(2,1)}), bf16[64,7,512]{2,1,0:T(8,128)(2,1)S(1)}, u32[]{:S(2)}, u32[]{:S(2)}) async-start(bf16[64,7,512]{2,1,0:T(8,128)(2,1)} %copy.20), calls=%async_computation | async-start | bytes 1048576 | tf_op jit(solution)/shard_map/all_to_all | solution.py:53
  26.3 1.1 convolution_convert_fusion.1
  27.4 16.0 %all-to-all-done = bf16[64,7,512]{2,1,0:T(8,128)(2,1)S(1)} async-done(((bf16[64,7,512]{2,1,0:T(8,128)(2,1)}), bf16[64,7,512]{2,1,0:T(8,128)(2,1)S(1)}, u32[]{:S(2)}, u32[]{:S(2)}) %all-to-all-start) | async-done | bytes 458784 | tf_op jit(solution)/shard_map/all_to_all | solution.py:53
  43.4 1.5 copy.21
  44.9 4.7 %all-to-all-start.2 = ((bf16[64,14,512]{2,1,0:T(8,128)(2,1)}), bf16[64,14,512]{2,1,0:T(8,128)(2,1)S(1)}, u32[]{:S(2)}, u32[]{:S(2)}) async-start(bf16[64,14,512]{2,1,0:T(8,128)(2,1)} %copy.21), calls=%async_computation.2 | async-start | bytes 2097152 | tf_op jit(solution)/shard_map/all_to_all | solution.py:53
  50.5 29.1 %all-to-all-done.2 = bf16[64,14,512]{2,1,0:T(8,128)(2,1)S(1)} async-done(((bf16[64,14,512]{2,1,0:T(8,128)(2,1)}), bf16[64,14,512]{2,1,0:T(8,128)(2,1)S(1)}, u32[]{:S(2)}, u32[]{:S(2)}) %all-to-all-start.2) | async-done | bytes 917536 | tf_op jit(solution)/shard_map/all_to_all | solution.py:53
  79.6 3.2 %stack.3 = bf16[8,448,512]{2,1,0:T(8,128)(2,1)} broadcast(bf16[448,512]{1,0:T(8,128)(2,1)} %stack_reshape.2), dimensions={1,2} | broadcast | bytes 4128768 | tf_op jit(solution)/shard_map/stack | solution.py:63
  82.8 6.5 %all-to-all-start.1 = ((bf16[8,448,512]{2,1,0:T(8,128)(2,1)}), bf16[8,448,512]{2,1,0:T(8,128)(2,1)}, u32[]{:S(2)}, u32[]{:S(2)}) async-start(bf16[8,448,512]{2,1,0:T(8,128)(2,1)} %stack.3), calls=%async_computation.1 | async-start | bytes 7340032 | tf_op jit(solution)/shard_map/all_to_all | solution.py:63
  91.0 81.8 %all-to-all-done.1 = bf16[8,448,512]{2,1,0:T(8,128)(2,1)} async-done(((bf16[8,448,512]{2,1,0:T(8,128)(2,1)}), bf16[8,448,512]{2,1,0:T(8,128)(2,1)}, u32[]{:S(2)}, u32[]{:S(2)}) %all-to-all-start.1) | async-done | bytes 3670048 | tf_op jit(solution)/shard_map/all_to_all | solution.py:63
  172.7 3.2 %fusion.4 = f32[256,512]{0,1:T(8,128)S(1)} fusion(bf16[3584,512]{1,0:T(8,128)(2,1)} %bitcast.1, bf16[1,1,256,3584]{3,2,1,0:T(8,128)(2,1)S(1)} %copy-done), kind=kOutput, calls=%fused_computation.9 | convolution fusion | flops 939524096 | bytes 6029312 | tf_op jit(solution)/shard_map/dot_general | solution.py:69
  176.1 3.0 fusion
  179.0 6.0 %copy.26 = bf16[3584,512]{1,0:T(8,128)(2,1)} copy(bf16[3584,512]{0,1:T(8,128)(2,1)} %fusion) | data formatting | bytes 7340032
  185.0 44.9 %reduce-scatter.4.cloned.1.call-done = bf16[448,512]{1,0:T(8,128)(2,1)} async-done(((bf16[3584,512]{1,0:T(8,128)(2,1)}), bf16[448,512]{1,0:T(8,128)(2,1)}) %reduce-scatter.4.cloned.1.call-update) | async-done | bytes 458768 | tf_op jit(solution)/shard_map/reduce_scatter | solution.py:74
  229.9 2.0 reshape.146
  231.9 31.4 %all_to_all.25 = bf16[64,7,512]{2,1,0:T(8,128)(2,1)S(1)} all-to-all(bf16[64,7,512]{2,1,0:T(8,128)(2,1)} %reshape.146), channel_id=1, replica_groups=mesh['dp'=8,'expert'=64] {'expert'}, dimensions={0} | all-to-all | bytes 917504 | tf_op jit(solution)/shard_map/all_to_all | solution.py:53
  263.6 1.1 copy.25
  264.6 6.6 %all-to-all-start.4 = ((bf16[64,7,512]{2,1,0:T(8,128)(2,1)}), bf16[64,7,512]{2,1,0:T(8,128)(2,1)}, u32[]{:S(2)}, u32[]{:S(2)}) async-start(bf16[64,7,512]{2,1,0:T(8,128)(2,1)} %copy.25), calls=%async_computation.4 | async-start | bytes 1048576 | tf_op jit(solution)/shard_map/all_to_all | solution.py:53
  272.3 1.6 convert_multiply_fusion
  273.9 2.4 mul.128
  276.3 2.3 mul.138
  278.6 12.5 %all-to-all-done.4 = bf16[64,7,512]{2,1,0:T(8,128)(2,1)} async-done(((bf16[64,7,512]{2,1,0:T(8,128)(2,1)}), bf16[64,7,512]{2,1,0:T(8,128)(2,1)}, u32[]{:S(2)}, u32[]{:S(2)}) %all-to-all-start.4) | async-done | bytes 458784 | tf_op jit(solution)/shard_map/all_to_all | solution.py:53
  291.1 2.1 reshape.149
  293.2 3.6 %subtract_convert_fusion = (bf16[1,448,512]{2,1,0:T(8,128)(2,1)}, f32[1,448,512]{2,1,0:T(8,128)}, f32[1,448,512]{2,1,0:T(8,128)}) fusion(f32[1,448,512]{2,1,0:T(8,128)S(1)} %copy-done.1, f32[1,448,512]{2,1,0:T(8,128)} %mul.128, f32[1,448,512]{2,1,0:T(8,128)} %reshape.149, f32[1,448,512]{2,1,0:T(8,128)} %mul.138), kind=kLoop, calls=%fused_computation.13 | loop fusion | flops 3211264 | bytes 5963776 | tf_op jit(solution)/shard_map/convert_element_type | solution.py:36
  (17 shorter events, 6.5 us)
Async XLA Ops:
  7.2 165.6 %copy-start = (bf16[1,1,256,3584]{3,2,1,0:T(8,128)(2,1)S(1)}, bf16[1,1,256,3584]{3,2,1,0:T(8,128)(2,1)}, u32[]{:S(2)}) copy-start(bf16[1,1,256,3584]{3,2,1,0:T(8,128)(2,1)} %param.12) | copy-start | bytes 5505028
  9.6 33.8 %all-to-all-start = ((bf16[64,7,512]{2,1,0:T(8,128)(2,1)}), bf16[64,7,512]{2,1,0:T(8,128)(2,1)S(1)}, u32[]{:S(2)}, u32[]{:S(2)}) async-start(bf16[64,7,512]{2,1,0:T(8,128)(2,1)} %copy.20), calls=%async_computation | async-start | bytes 1048576 | tf_op jit(solution)/shard_map/all_to_all | solution.py:53
  44.9 34.7 %all-to-all-start.2 = ((bf16[64,14,512]{2,1,0:T(8,128)(2,1)}), bf16[64,14,512]{2,1,0:T(8,128)(2,1)S(1)}, u32[]{:S(2)}, u32[]{:S(2)}) async-start(bf16[64,14,512]{2,1,0:T(8,128)(2,1)} %copy.21), calls=%async_computation.2 | async-start | bytes 2097152 | tf_op jit(solution)/shard_map/all_to_all | solution.py:53
  82.8 90.0 %all-to-all-start.1 = ((bf16[8,448,512]{2,1,0:T(8,128)(2,1)}), bf16[8,448,512]{2,1,0:T(8,128)(2,1)}, u32[]{:S(2)}, u32[]{:S(2)}) async-start(bf16[8,448,512]{2,1,0:T(8,128)(2,1)} %stack.3), calls=%async_computation.1 | async-start | bytes 7340032 | tf_op jit(solution)/shard_map/all_to_all | solution.py:63
  89.3 140.6 %reduce-scatter.4.cloned.1.call-start = ((), (), s32[]{:S(2)}) async-start(), calls=%async_computation.6 | async-start | bytes 4128768 | tf_op jit(solution)/shard_map/reduce_scatter | solution.py:74
  185.0 78.2 %copy-start.2 = (s32[64]{0:T(128)S(1)}, s32[64]{0:T(128)}, u32[]{:S(2)}) copy-start(s32[64]{0:T(128)} %param.10) | copy-start | bytes 772
  264.6 26.5 %all-to-all-start.4 = ((bf16[64,7,512]{2,1,0:T(8,128)(2,1)}), bf16[64,7,512]{2,1,0:T(8,128)(2,1)}, u32[]{:S(2)}, u32[]{:S(2)}) async-start(bf16[64,7,512]{2,1,0:T(8,128)(2,1)} %copy.25), calls=%async_computation.4 | async-start | bytes 1048576 | tf_op jit(solution)/shard_map/all_to_all | solution.py:53
  273.9 19.3 %copy-start.1 = (f32[1,448,512]{2,1,0:T(8,128)S(1)}, f32[1,448,512]{2,1,0:T(8,128)}, u32[]{:S(2)}) copy-start(f32[1,448,512]{2,1,0:T(8,128)} %reshape.147) | copy-start | bytes 2752516
Sparse Core Ops, SparseCore 0:
  185.2 44.6 reduce-scatter.3
